TPU v7x, 32 devices: a whole 2x2x4 slice. The times are simulated.
32 devices in a mesh: groups: 2 (over x), rows: 8 (over z, y), cols: 2 (over core).
Axes of the slice: x: 2, y: 2, z: 4, core: 2. Of those that a mesh axis runs over, the one named last changes fastest.
Arguments:
- feature_table: float32 [32768, 1024], P(('groups', 'rows'), 'cols'), parts along dimension 0, may hold values from -6 to 6
- own_features: float32 [512, 1024], P(('groups', 'rows'), 'cols'), parts along dimension 0, may hold values from -6 to 6
- neighbor_ids: int32 [512, 50], P(('groups', 'rows')), parts along dimension 0, may hold values from 0 to 16383, as said below
- importance: float32 [512, 50], P(('groups', 'rows')), parts along dimension 0, may hold values from 0.5 to 5
- w_self: bfloat16 [1024, 1024], P('cols'), may hold values from -0.1875 to 0.1875
- w_pool: bfloat16 [1024, 1024], P('cols'), may hold values from -0.1875 to 0.1875
- bias: float32 [1024], replicated, may hold values from -6 to 6
Outputs:
- embeddings: float32 [512, 1024], P(('groups', 'rows'), 'cols'), parts along dimension 0
There are 2 independent parts, one for each index of `groups`. A program takes and returns all parts, laid end to end along the dimension named above; an argument that names none is the same for every part. Nothing has to cross between parts.
Inputs may be any that keep to these rules, and one draw needn't show every extreme that they name: `neighbor_ids`: ids of sampled neighbors in the group's table, repeats allowed. In each aligned block of 16 targets, at most 160 ids fall in any one range [k * 2048, (k + 1) * 2048), and one such range holds exactly 160.
All inputs are finite; a program needn't handle non-finite values.
Results may differ from a plain program's by a relative error of at most 0.0017.
Values may be sent and summed in bfloat16 or wider, within the bound.
A program may use at most 64 MiB of HBM per device.

v0:
```python
from functools import partial

import jax
import jax.numpy as jnp
from jax import lax
from jax.sharding import PartitionSpec as P

NEIGH = 50
TGT_DEV = 16


def request_slots(id_block, share_block, owners, capacity, rows_dev):
    targets = id_block.shape[0]
    neighbors = id_block.shape[1]
    flat_ids = id_block.reshape(-1)
    owner_of = flat_ids // rows_dev
    local_row = flat_ids - owner_of * rows_dev
    target_of = jnp.arange(targets * neighbors, dtype=jnp.int32) // neighbors
    onehot = (owner_of[:, None] == jnp.arange(owners, dtype=jnp.int32)[None, :]).astype(jnp.int32)
    slot_rank = jnp.sum((jnp.cumsum(onehot, axis=0) - onehot) * onehot, axis=1)
    sending = jnp.zeros((owners, capacity), jnp.int32).at[owner_of, slot_rank].set(local_row)
    packed = (
        jnp.zeros((owners, capacity), jnp.int32)
        .at[owner_of, slot_rank]
        .set(local_row * targets + target_of)
    )
    slot_weight = (
        jnp.zeros((owners, capacity), jnp.float32)
        .at[owner_of, slot_rank]
        .set(share_block.reshape(-1))
    )
    return (owner_of, slot_rank, sending, packed, slot_weight)


def plan_requests(id_rows, shares, blocks, owners, capacity, rows_dev):
    targets = id_rows.shape[0] // blocks
    neighbors = id_rows.shape[1]
    per_block = targets * neighbors
    owner_of, slot_rank, sending, packed, slot_weight = jax.vmap(
        partial(request_slots, owners=owners, capacity=capacity, rows_dev=rows_dev)
    )(id_rows.reshape(blocks, targets, neighbors), shares.reshape(blocks, targets, neighbors))
    block_of = jnp.arange(blocks, dtype=jnp.int32)[:, None]
    column = owner_of * (blocks * capacity) + block_of * capacity + slot_rank
    row_index = block_of * targets + jnp.arange(per_block, dtype=jnp.int32)[None, :] // neighbors
    pool_matrix = (
        jnp.zeros((blocks * targets, owners * blocks * capacity), jnp.float32)
        .at[row_index.reshape(-1), column.reshape(-1)]
        .add(shares.reshape(-1))
    )
    outgoing = jnp.transpose(sending, (1, 0, 2)).reshape(owners, blocks * capacity)
    packed_out = jnp.transpose(packed, (1, 0, 2)).reshape(owners, blocks * capacity)
    weight_out = jnp.transpose(slot_weight, (1, 0, 2)).reshape(owners, blocks * capacity)
    return (pool_matrix, outgoing, packed_out, weight_out)


def finish_rows(preact):
    hidden = jnp.maximum(preact, 0.0)
    return hidden * lax.rsqrt(jnp.mean(hidden * hidden, axis=1, keepdims=True) + 1e-06)


def body(feature_table, own_features, neighbor_ids, importance, w_self, w_pool, bias):
    rows_dev, width_half = feature_table.shape
    owners = lax.axis_size("rows")
    col_count = lax.axis_size("cols")
    capacity = TGT_DEV * NEIGH * 8 // (5 * owners)
    shares = importance / jnp.sum(importance, axis=1, keepdims=True)
    own_round = own_features.astype(jnp.bfloat16)
    pool_matrix, outgoing, packed_out, weight_out = plan_requests(
        neighbor_ids, shares, col_count, owners, capacity, rows_dev
    )
    found = jnp.take(
        feature_table,
        lax.all_to_all(outgoing, "rows", split_axis=0, concat_axis=0, tiled=True),
        axis=0,
    )
    arrived = lax.all_to_all(
        found.astype(jnp.bfloat16), "rows", split_axis=0, concat_axis=0, tiled=True
    ).astype(found.dtype)
    pooled = jnp.dot(
        pool_matrix,
        arrived.reshape(-1, width_half),
        precision=lax.Precision.HIGHEST,
        preferred_element_type=jnp.float32,
    )
    partial_sums = jnp.dot(own_round, w_self, preferred_element_type=jnp.float32) + jnp.dot(
        pooled.astype(jnp.bfloat16), w_pool, preferred_element_type=jnp.float32
    )
    column_start = lax.axis_index("cols") * width_half
    preact = lax.psum(partial_sums, "cols") + bias
    embedded = finish_rows(preact)
    return lax.dynamic_slice_in_dim(embedded, column_start, width_half, 1)


def solution(mesh):
    placed = (
        P(("groups", "rows"), "cols"),
        P(("groups", "rows"), "cols"),
        P(("groups", "rows"), None),
        P(("groups", "rows"), None),
        P("cols", None),
        P("cols", None),
        P(),
    )
    return jax.shard_map(
        body, mesh=mesh, in_specs=placed, out_specs=P(("groups", "rows"), "cols"), check_vma=False
    )
```

profile of v0, /device:TPU:0, one launch (start us, length us, event | category | flops | bytes accessed | tf_op | source)
XLA Modules:
  0.0 143.6 jit_solution(3626495202267903380)
XLA Ops:
  6.5 0.0 copy-start
  6.5 0.9 reshape_reshape.8
  7.4 0.8 reshape_reshape.9
  8.3 4.0 %reduce-window.6 = s32[2,8,7,128]{3,1,2,0:T(8,128)S(1)} reduce-window(s32[2,8,7,128]{3,1,2,0:T(8,128)S(1)} %convert_bitcast_fusion, s32[]{:T(128)} %constant.33.clone.1), window={size=1x1x1x128 pad=0_0x0_0x0_0x127_0}, to_apply=%region_0.0 | reduce-window | flops 1820672 | bytes 114692 | tf_op jit(solution)/shard_map/reduce-window
  12.3 0.1 slice.14
  12.4 0.2 copy.15
  12.5 0.1 add_bitcast_fusion
  12.7 0.7 multiply_reduce_fusion.1
  13.5 0.8 and_reduce_fusion
  14.2 0.1 reshape.362
  14.3 0.1 reshape.364
  14.4 8.8 %scatter_custom_fusion.1 = s32[2560]{0:T(1024)S(1)} fusion(s32[1600]{0:T(1024)S(1)} %reshape.362, s32[1600]{0:T(1024)S(1)} %reshape.364, s32[]{:T(128)} %constant.33.clone.1), kind=kCustom, calls=%fused_computation.54 | custom fusion | bytes 10244
  23.2 0.1 reshape.346
  23.3 0.1 all_to_all.18
  23.4 13.6 %all_to_all.21 = s32[8,1,320]{2,1,0:T(1,128)S(1)} all-to-all(s32[8,1,320]{2,1,0:T(1,128)S(1)} %all_to_all.18), channel_id=1, replica_groups=mesh['groups'=2,'rows'=8,'cols'=2] {'rows'}, dimensions={0} | all-to-all | bytes 20480 | tf_op jit(solution)/shard_map/all_to_all | solution.py:73
  37.1 0.1 reshape.350
  37.2 10.5 %gather_fusion = bf16[2560,512]{1,0:T(8,128)(2,1)} fusion(f32[2048,512]{1,0:T(8,128)} %param.7, s32[3072]{0:T(1024)S(1)} %pad_clamp_fusion), kind=kCustom, calls=%fused_computation | custom fusion | bytes 5253120 | tf_op jit(solution)/shard_map/jit(_take)/gather | solution.py:71
  47.7 3.2 %select_convert_fusion = bf16[8,320,512]{2,1,0:T(8,128)(2,1)} fusion(bf16[8,320,512]{2,1,0:T(8,128)(2,1)} %bitcast.25, pred[8,320]{1,0:T(8,128)(4,1)S(1)} %compare_and_fusion), kind=kLoop, calls=%fused_computation.3 | loop fusion | flops 1310720 | bytes 5245440 | tf_op jit(solution)/shard_map/convert_element_type | solution.py:77
  50.9 0.0 copy-start.2
  50.9 0.0 copy-start.4
  50.9 0.0 copy-start.7
  50.9 0.0 copy-start.6
  50.9 0.0 copy-start.3
  50.9 4.5 %all-to-all-start.1 = ((bf16[8,320,512]{2,1,0:T(8,128)(2,1)}), bf16[8,320,512]{2,1,0:T(8,128)(2,1)}, u32[]{:S(2)}, u32[]{:S(2)}) async-start(bf16[8,320,512]{2,1,0:T(8,128)(2,1)} %select_convert_fusion), calls=%async_computation.1 | async-start | bytes 5242880 | tf_op jit(solution)/shard_map/all_to_all | solution.py:76
  55.5 0.0 all-reduce.3.cloned.1.call-start
  55.5 0.1 reduce_sum.32
  55.6 0.0 copy-done.2
  55.6 0.1 reshape_reshape.7
  55.8 0.1 broadcast_add_fusion
  55.8 0.1 add.183
  55.9 0.1 add.186
  56.0 0.1 add.187
  56.1 0.0 copy-done.4
  56.1 0.1 reduce_sum.33
  56.2 0.1 broadcast_divide_fusion
  56.3 0.1 reshape.358
  56.4 0.1 compare_select_fusion.1
  56.5 0.0 copy-done.7
  56.5 0.1 multiply_reduce_fusion.2
  56.6 0.0 copy-done.6
  56.6 0.0 copy-start.1
  56.6 0.1 and_reduce_fusion.1
  56.7 10.1 %scatter_custom_fusion = f32[81920]{0:T(1024)S(1)} fusion(s32[1600]{0:T(1024)S(1)} %broadcast_select_fusion, f32[1600]{0:T(1024)S(1)} %reshape.358, f32[]{:T(128)} %constant.24.clone.1), kind=kCustom, calls=%fused_computation.6 | custom fusion | flops 1600 | bytes 327684
  66.8 0.1 reshape.342
  66.9 0.0 copy-done
  66.9 0.0 copy-done.3
  66.9 0.0 copy-start.5
  66.9 0.3 fusion.4
  67.2 46.6 %all-to-all-done.1 = bf16[8,320,512]{2,1,0:T(8,128)(2,1)} async-done(((bf16[8,320,512]{2,1,0:T(8,128)(2,1)}), bf16[8,320,512]{2,1,0:T(8,128)(2,1)}, u32[]{:S(2)}, u32[]{:S(2)}) %all-to-all-start.1) | async-done | bytes 2621472 | tf_op jit(solution)/shard_map/all_to_all | solution.py:76
  113.8 3.1 %convolution_convert_fusion = bf16[32,512]{1,0:T(8,128)(2,1)S(1)} fusion(f32[32,2560]{1,0:T(8,128)S(1)} %reshape.342, bf16[2560,512]{1,0:T(8,128)(2,1)} %bitcast.8), kind=kOutput, calls=%fused_computation.5 | convolution fusion | flops 503332864 | bytes 2981888 | tf_op jit(solution)/shard_map/dot_general | solution.py:79
  116.9 0.0 copy-done.1
  116.9 0.9 convolution_add_fusion
  117.8 0.0 all-reduce.3.cloned.1.call-update
  117.9 17.1 %all-reduce.3.cloned.1.call-done = f32[32,1024]{1,0:T(8,128)} async-done(((f32[32,1024]{1,0:T(8,128)}), f32[32,1024]{1,0:T(8,128)}) %all-reduce.3.cloned.1.call-update) | async-done | bytes 131088 | tf_op jit(solution)/shard_map/psum | solution.py:89
  135.0 0.0 copy-done.5
  135.0 1.0 multiply_reduce_fusion
  136.0 0.7 dynamic-slice_multiply_fusion
  (19 shorter events, 0.2 us)
Async XLA Ops:
  6.5 60.3 %copy-start = (bf16[512,1024]{1,0:T(8,128)(2,1)S(1)}, bf16[512,1024]{1,0:T(8,128)(2,1)}, u32[]{:S(2)}) copy-start(bf16[512,1024]{1,0:T(8,128)(2,1)} %param.11) | copy-start | bytes 3145732
  50.9 4.7 %copy-start.2 = (s32[32,50]{1,0:T(8,128)S(1)}, s32[32,50]{1,0:T(8,128)}, u32[]{:S(2)}) copy-start(s32[32,50]{1,0:T(8,128)} %param.9) | copy-start | bytes 19204
  50.9 5.2 %copy-start.4 = (f32[32,50]{1,0:T(8,128)S(1)}, f32[32,50]{1,0:T(8,128)}, u32[]{:S(2)}) copy-start(f32[32,50]{1,0:T(8,128)} %param.10) | copy-start | bytes 19204
  50.9 5.5 %copy-start.7 = (s32[2]{0:T(128)S(1)}, s32[2]{0:T(128)}, u32[]{:S(2)}) copy-start(s32[2]{0:T(128)} %constant.81) | copy-start | bytes 28
  50.9 5.6 %copy-start.6 = (s32[2]{0:T(128)S(1)}, s32[2]{0:T(128)}, u32[]{:S(2)}) copy-start(s32[2]{0:T(128)} %constant.84) | copy-start | bytes 28
  50.9 15.9 %copy-start.3 = (f32[32,512]{1,0:T(8,128)S(1)}, f32[32,512]{1,0:T(8,128)}, u32[]{:S(2)}) copy-start(f32[32,512]{1,0:T(8,128)} %param.8) | copy-start | bytes 196612
  50.9 62.9 %all-to-all-start.1 = ((bf16[8,320,512]{2,1,0:T(8,128)(2,1)}), bf16[8,320,512]{2,1,0:T(8,128)(2,1)}, u32[]{:S(2)}, u32[]{:S(2)}) async-start(bf16[8,320,512]{2,1,0:T(8,128)(2,1)} %select_convert_fusion), calls=%async_computation.1 | async-start | bytes 5242880 | tf_op jit(solution)/shard_map/all_to_all | solution.py:76
  55.5 79.5 %all-reduce.3.cloned.1.call-start = ((), (), s32[]{:S(2)}) async-start(), calls=%async_computation.2 | async-start | bytes 262144 | tf_op jit(solution)/shard_map/psum | solution.py:89
  56.6 60.3 %copy-start.1 = (bf16[512,1024]{1,0:T(8,128)(2,1)S(1)}, bf16[512,1024]{1,0:T(8,128)(2,1)}, u32[]{:S(2)}) copy-start(bf16[512,1024]{1,0:T(8,128)(2,1)} %param.12) | copy-start | bytes 3145732
  66.9 68.1 %copy-start.5 = (f32[1024]{0:T(1024)S(1)}, f32[1024]{0:T(1024)}, u32[]{:S(2)}) copy-start(f32[1024]{0:T(1024)} %param.13) | copy-start | bytes 12292
Sparse Core Ops, SparseCore 0:
  118.0 16.9 all-reduce.2
where the time goes:
time: 144 us
  waiting for transfers between devices  63.8 us (44%)
  local copies, waits for them, and re-layouts  22.4 us (16%)
  other arithmetic  21.3 us (15%)
  blocking collectives  13.6 us (9%)
  between operations  13.6 us (9%)
  starting transfers between devices  4.58 us (3%)
  matrix products  4.29 us (3%)
    all_to_all x1, waiting for transfers between devices, body(): lax.all_to_all(found.astype(jnp.bfloat16), 'rows', split_axis=0, concat_a...  46.6 us
    psum x1, waiting for transfers between devices, body(): preact = lax.psum(partial_sums, 'cols') + bias  17.1 us
    all_to_all x1, blocking collectives, body(): lax.all_to_all(outgoing, 'rows', split_axis=0, concat_axis=0, tiled=True)  13.6 us
    unnamed x7, other arithmetic  11.8 us
    gather x1, local copies, waits for them, and re-layouts, body(): jnp.take(feature_table, lax.all_to_all(outgoing, 'rows', split_axis=0, co...  10.5 us
    unnamed x19, local copies, waits for them, and re-layouts  8.94 us
    all_to_all x1, starting transfers between devices, body(): lax.all_to_all(found.astype(jnp.bfloat16), 'rows', split_axis=0, concat_a...  4.54 us
    another operation x4, other arithmetic  4.06 us
  transfers between devices with their start and end apart: 2, of which 2 were waited for; matrix products, arithmetic and copies ran while one was open for 8% of the time, Pallas kernels for 0%

commit v1 on v0

v1 whole, which is shorter than its diff:
```python
from functools import partial

import jax
import jax.numpy as jnp
from jax import lax
from jax.experimental import pallas as pl
from jax.experimental.pallas import tpu as pltpu
from jax.sharding import PartitionSpec as P

MESH = pl.DeviceIdType.MESH
LANES = 128
HALF = 64
SUB = 8


def kernel(
    n,
    peers_chunk,
    ids_ref,
    imp_ref,
    own_ref,
    bias_ref,
    table_hbm,
    ws_hbm,
    wp_hbm,
    out_ref,
    table_v,
    table_b,
    ws_v,
    wp_v,
    pack_send,
    packs,
    wmat,
    mine,
    psend,
    precv,
    fsend,
    frecv,
    local_sem,
    pack_ssem,
    pack_rsem,
    part_ssem,
    part_rsem,
    fin_sem,
):
    me = lax.axis_index("rows")
    col = lax.axis_index("cols")
    targets, neigh = ids_ref.shape
    rows_dev, width = table_v.shape
    groups = targets // SUB
    half_rows = targets // 2
    hi_count = rows_dev // LANES

    barrier = pltpu.get_barrier_semaphore()

    def greet(d, carry):
        pl.semaphore_signal(
            barrier, inc=1, device_id={"rows": lax.rem(me + d, n)}, device_id_type=MESH
        )
        return carry

    lax.fori_loop(1, n, greet, 0)
    pl.semaphore_signal(barrier, inc=1, device_id={"cols": 1 - col}, device_id_type=MESH)

    copies = (
        pltpu.make_async_copy(table_hbm, table_v, local_sem.at[0]),
        pltpu.make_async_copy(ws_hbm, ws_v, local_sem.at[1]),
        pltpu.make_async_copy(wp_hbm, wp_v, local_sem.at[2]),
    )
    for c in copies:
        c.start()

    pack_send[...] = jnp.full(pack_send.shape, -1.0, jnp.float32)
    for g in range(groups):
        for part in range(2):
            src = pl.ds(SUB * g + 4 * part, 4)
            dst = pl.ds(HALF * part, neigh)
            pack_send[pl.ds(4 * g, 4), dst] = ids_ref[src, :].astype(jnp.float32)
            pack_send[pl.ds(half_rows + 4 * g, 4), dst] = imp_ref[src, :]
    packs[0] = pack_send[...]

    pl.semaphore_wait(barrier, n)

    def pack_copy(d):
        return pltpu.make_async_remote_copy(
            src_ref=pack_send,
            dst_ref=packs.at[d],
            send_sem=pack_ssem.at[d],
            recv_sem=pack_rsem.at[d],
            device_id={"rows": lax.rem(me + d, n)},
            device_id_type=MESH,
        )

    def start_pack(d, carry):
        pack_copy(d).start()
        return carry

    lax.fori_loop(1, n, start_pack, 0)

    copies[0].wait()
    table_b[...] = table_v[...].astype(jnp.bfloat16)
    copies[1].wait()
    fsend[...] = jnp.dot(
        own_ref[...].astype(jnp.bfloat16), ws_v[...], preferred_element_type=jnp.float32
    )

    row_iota = lax.broadcasted_iota(jnp.int32, (LANES, LANES), 0).astype(jnp.float32)
    key_iota = lax.broadcasted_iota(jnp.int32, (hi_count * SUB, LANES), 0).astype(jnp.float32)
    lane = lax.broadcasted_iota(jnp.int32, (half_rows, LANES), 1)
    prow = lax.broadcasted_iota(jnp.int32, (half_rows, LANES), 0)
    t_of = (lax.rem(prow, 4) + jnp.where(lane >= HALF, 4, 0)).astype(jnp.float32)
    base = (me * rows_dev).astype(jnp.float32)

    def build(d, slot):
        ids = packs[d, pl.ds(0, half_rows), :]
        weight = packs[d, pl.ds(half_rows, half_rows), :]
        rel = ids - base
        valid = jnp.logical_and(rel >= 0.0, rel < float(rows_dev))
        high = jnp.floor(rel * (1.0 / LANES))
        low = rel - high * LANES
        key = jnp.where(valid, high * SUB + t_of, -1.0)
        for g in range(groups):
            lhs, rhs = [], []
            for c in range(4):
                r = 4 * g + c
                lhs.append(
                    jnp.where(key_iota == key[r : r + 1, :], weight[r : r + 1, :], 0.0).astype(
                        jnp.bfloat16
                    )
                )
                rhs.append(
                    jnp.where(row_iota == low[r : r + 1, :], 1.0, 0.0).astype(jnp.bfloat16)
                )
            block = lax.dot_general(
                jnp.concatenate(lhs, axis=1),
                jnp.concatenate(rhs, axis=1),
                (((1,), (1,)), ((), ())),
                preferred_element_type=jnp.float32,
            )
            row = pl.multiple_of(slot * targets + SUB * g, SUB)
            for h in range(hi_count):
                wmat[pl.ds(row, SUB), pl.ds(h * LANES, LANES)] = block[h * SUB : (h + 1) * SUB, :]

    def part_copy(d):
        return pltpu.make_async_remote_copy(
            src_ref=psend.at[d],
            dst_ref=precv.at[d],
            send_sem=part_ssem.at[d],
            recv_sem=part_rsem.at[d],
            device_id={"rows": lax.rem(me - d + n, n)},
            device_id_type=MESH,
        )

    def chunk(first, has_own):
        def one(s, carry):
            d = first + s
            pack_copy(d).wait_recv()
            build(d, s)
            return carry

        if has_own:
            build(0, 0)
        lax.fori_loop(1 if has_own else 0, peers_chunk, one, 0)
        sums = jnp.dot(
            wmat[...].astype(jnp.bfloat16), table_b[...], preferred_element_type=jnp.float32
        )
        for s in range(peers_chunk):
            rows = sums[s * targets : (s + 1) * targets, :]
            if has_own and s == 0:
                mine[...] = rows
            else:
                psend[first + s] = rows.astype(jnp.bfloat16)
                part_copy(first + s).start()

    chunk(0, True)

    def later(i, carry):
        chunk(i * peers_chunk, False)
        return carry

    lax.fori_loop(1, n // peers_chunk, later, 0)

    def collect(d, carry):
        part_copy(d).wait_recv()
        mine[...] += precv[d].astype(jnp.float32)
        return carry

    lax.fori_loop(1, n, collect, 0)
    pooled = mine[...] / jnp.sum(imp_ref[...], axis=1, keepdims=True)
    copies[2].wait()
    fsend[...] += jnp.dot(
        pooled.astype(jnp.bfloat16), wp_v[...], preferred_element_type=jnp.float32
    )
    swap = pltpu.make_async_remote_copy(
        src_ref=fsend,
        dst_ref=frecv,
        send_sem=fin_sem.at[0],
        recv_sem=fin_sem.at[1],
        device_id={"cols": 1 - col},
        device_id_type=MESH,
    )
    swap.start()
    swap.wait_recv()
    hidden = jnp.maximum(fsend[...] + frecv[...] + bias_ref[...], 0.0)
    scale = lax.rsqrt(jnp.mean(hidden * hidden, axis=1, keepdims=True) + 1e-06)
    half = jnp.where(col == 0, hidden[:, :width], hidden[:, width:])
    out_ref[...] = half * scale

    swap.wait_send()

    def drain(d, carry):
        pack_copy(d).wait_send()
        part_copy(d).wait_send()
        return carry

    lax.fori_loop(1, n, drain, 0)


def body(feature_table, own_features, neighbor_ids, importance, w_self, w_pool, bias):
    rows_dev, width = feature_table.shape
    targets, neigh = neighbor_ids.shape
    n = lax.axis_size("rows")
    full = w_self.shape[1]
    assert lax.axis_size("cols") == 2 and neigh <= HALF and targets % 16 == 0
    peers_chunk = 4 if n % 4 == 0 else 1
    vmem = pl.BlockSpec(memory_space=pltpu.VMEM)
    hbm = pl.BlockSpec(memory_space=pl.ANY)
    return pl.pallas_call(
        partial(kernel, n, peers_chunk),
        out_shape=jax.ShapeDtypeStruct((targets, width), jnp.float32),
        in_specs=[vmem, vmem, vmem, vmem, hbm, hbm, hbm],
        out_specs=vmem,
        scratch_shapes=[
            pltpu.VMEM((rows_dev, width), jnp.float32),
            pltpu.VMEM((rows_dev, width), jnp.bfloat16),
            pltpu.VMEM(w_self.shape, jnp.bfloat16),
            pltpu.VMEM(w_pool.shape, jnp.bfloat16),
            pltpu.VMEM((targets, LANES), jnp.float32),
            pltpu.VMEM((n, targets, LANES), jnp.float32),
            pltpu.VMEM((peers_chunk * targets, rows_dev), jnp.float32),
            pltpu.VMEM((targets, width), jnp.float32),
            pltpu.VMEM((n, targets, width), jnp.bfloat16),
            pltpu.VMEM((n, targets, width), jnp.bfloat16),
            pltpu.VMEM((targets, full), jnp.float32),
            pltpu.VMEM((targets, full), jnp.float32),
            pltpu.SemaphoreType.DMA((3,)),
            pltpu.SemaphoreType.DMA((n,)),
            pltpu.SemaphoreType.DMA((n,)),
            pltpu.SemaphoreType.DMA((n,)),
            pltpu.SemaphoreType.DMA((n,)),
            pltpu.SemaphoreType.DMA((2,)),
        ],
        compiler_params=pltpu.CompilerParams(collective_id=0, has_side_effects=True),
    )(
        neighbor_ids,
        importance,
        own_features,
        bias.reshape(1, full),
        feature_table,
        w_self,
        w_pool,
    )


def solution(mesh):
    placed = (
        P(("groups", "rows"), "cols"),
        P(("groups", "rows"), "cols"),
        P(("groups", "rows"), None),
        P(("groups", "rows"), None),
        P("cols", None),
        P("cols", None),
        P(),
    )
    return jax.shard_map(
        body, mesh=mesh, in_specs=placed, out_specs=P(("groups", "rows"), "cols"), check_vma=False
    )
```

time: 144 us -> 22.9 us (0.16)
  waiting for transfers between devices: 63.8 us -> 0 us
  Pallas kernels: 0 us -> 21.3 us
  other arithmetic: 21.3 us -> 0 us
  local copies, waits for them, and re-layouts: 22.4 us -> 1.47 us
  blocking collectives: 13.6 us -> 0 us
  between operations: 13.6 us -> 0.01 us
  starting transfers between devices: 4.58 us -> 0 us
  matrix products: 4.29 us -> 0 us
    all_to_all x1 -> x0, waiting for transfers between devices: 46.6 us -> none  [body(): lax.all_to_all(found.astype(jnp.bfloat16), 'rows', split_axis=0, concat_a...]
    pallas_call x0 -> x1, Pallas kernels: none -> 21.3 us  [body(): pl.pallas_call(partial(kernel, n, peers_chunk), out_shape=jax.ShapeDtypeS...]
    psum x1 -> x0, waiting for transfers between devices: 17.1 us -> none  [body(): preact = lax.psum(partial_sums, 'cols') + bias]
    all_to_all x1 -> x0, blocking collectives: 13.6 us -> none  [body(): lax.all_to_all(outgoing, 'rows', split_axis=0, concat_axis=0, tiled=True)]
    unnamed x7 -> x0, other arithmetic: 11.8 us -> none
    gather x1 -> x0, local copies, waits for them, and re-layouts: 10.5 us -> none  [body(): jnp.take(feature_table, lax.all_to_all(outgoing, 'rows', split_axis=0, co...]
    unnamed x19 -> x1, local copies, waits for them, and re-layouts: 8.94 us -> 1.47 us
    all_to_all x1 -> x0, starting transfers between devices: 4.54 us -> none  [body(): lax.all_to_all(found.astype(jnp.bfloat16), 'rows', split_axis=0, concat_a...]
  transfers between devices with their start and end apart: 2 -> 0, of which waited for: 2 -> 0; matrix products, arithmetic and copies ran while one was open for 8% -> 0% of each run, Pallas kernels for 0% -> 0%
where the time goes in v1:
time: 22.9 us; the launch traced here: 22.7 us
  Pallas kernels  21.3 us (93%)
  local copies, waits for them, and re-layouts  1.47 us (6%)
    pallas_call x1, Pallas kernels, body(): pl.pallas_call(partial(kernel, n, peers_chunk), out_shape=jax.ShapeDtypeS...  21.3 us
    unnamed x1, local copies, waits for them, and re-layouts  1.47 us

profile of v1, /device:TPU:0, one launch (start us, length us, event | category | flops | bytes accessed | tf_op | source)
XLA Modules:
  0.0 22.7 jit_solution(10156684443493181310)
XLA Ops:
  0.0 21.3 %shard_map.73 = f32[32,512]{1,0:T(8,128)} custom-call(s32[32,50]{1,0:T(8,128)} %ids_ref.1, f32[32,50]{1,0:T(8,128)} %imp_ref.1, f32[32,512]{1,0:T(8,128)} %own_ref.1, f32[1,1024]{1,0:T(1,128)} %bitcast.1, f32[2048,512]{1,0:T(8,128)} %table_hbm.1, bf16[512,1024]{1,0:T(8,128)(2,1)} %ws_hbm.1, bf16[512,1024]{1,0:T(8,128)(2,1)} %wp_hbm.1), custom_call_target="tpu_custom_call" | custom-call | tf_op jit(solution)/shard_map/pallas_call | solution.py:228
  21.3 1.5 %copy.9 = f32[32,512]{1,0:T(8,128)} copy(f32[32,512]{1,0:T(8,128)} %shard_map.73) | data formatting | bytes 131072

commit v2 on v1

--- a/solution.py
+++ b/solution.py
@@ -11,23 +11,29 @@
 LANES = 128
 HALF = 64
 SUB = 8
+IMP_SCALE = 6000.0
 
 
 def kernel(
     n,
     peers_chunk,
+    ids_hbm,
+    imp_hbm,
+    own_hbm,
+    bias_hbm,
+    table_hbm,
+    ws_hbm,
+    wp_hbm,
+    out_ref,
     ids_ref,
     imp_ref,
     own_ref,
     bias_ref,
-    table_hbm,
-    ws_hbm,
-    wp_hbm,
-    out_ref,
     table_v,
     table_b,
     ws_v,
     wp_v,
+    pack_in,
     pack_send,
     packs,
     wmat,
@@ -53,53 +59,85 @@
 
     barrier = pltpu.get_barrier_semaphore()
 
+    def partner(k):
+        peer, bit = me, 1
+        while bit < n:
+            peer = peer + lax.rem(k // bit, 2) * (1 - 2 * lax.rem(me // bit, 2)) * bit
+            bit *= 2
+        return peer
+
     def greet(d, carry):
         pl.semaphore_signal(
-            barrier, inc=1, device_id={"rows": lax.rem(me + d, n)}, device_id_type=MESH
+            barrier, inc=1, device_id={"rows": partner(d)}, device_id_type=MESH
         )
         return carry
 
     lax.fori_loop(1, n, greet, 0)
     pl.semaphore_signal(barrier, inc=1, device_id={"cols": 1 - col}, device_id_type=MESH)
 
-    copies = (
-        pltpu.make_async_copy(table_hbm, table_v, local_sem.at[0]),
-        pltpu.make_async_copy(ws_hbm, ws_v, local_sem.at[1]),
-        pltpu.make_async_copy(wp_hbm, wp_v, local_sem.at[2]),
+    copies = tuple(
+        pltpu.make_async_copy(src, dst, local_sem.at[i])
+        for i, (src, dst) in enumerate(
+            (
+                (ids_hbm, ids_ref),
+                (imp_hbm, imp_ref),
+                (own_hbm, own_ref),
+                (bias_hbm, bias_ref),
+                (table_hbm, table_v),
+                (ws_hbm, ws_v),
+                (wp_hbm, wp_v),
+            )
+        )
     )
     for c in copies:
         c.start()
-
-    pack_send[...] = jnp.full(pack_send.shape, -1.0, jnp.float32)
+    copies[0].wait()
+    copies[1].wait()
+
+    pack_in[...] = jnp.full(pack_in.shape, -1, jnp.int32)
     for g in range(groups):
         for part in range(2):
             src = pl.ds(SUB * g + 4 * part, 4)
             dst = pl.ds(HALF * part, neigh)
-            pack_send[pl.ds(4 * g, 4), dst] = ids_ref[src, :].astype(jnp.float32)
-            pack_send[pl.ds(half_rows + 4 * g, 4), dst] = imp_ref[src, :]
-    packs[0] = pack_send[...]
+            pack_in[pl.ds(4 * g, 4), dst] = ids_ref[src, :]
+            pack_in[pl.ds(half_rows + 4 * g, 4), dst] = jnp.round(
+                imp_ref[src, :] * IMP_SCALE
+            ).astype(jnp.int32)
+
+    def pack_for(k, carry):
+        local = pack_in[pl.ds(0, half_rows), :] - partner(k) * rows_dev
+        local = jnp.where(jnp.logical_and(local >= 0, local < rows_dev), local, -1)
+        pack_send[k, pl.ds(0, half_rows), :] = local.astype(jnp.int16)
+        pack_send[k, pl.ds(half_rows, half_rows), :] = pack_in[
+            pl.ds(half_rows, half_rows), :
+        ].astype(jnp.int16)
+        return carry
+
+    lax.fori_loop(0, n, pack_for, 0)
+    packs[0] = pack_send[0]
 
     pl.semaphore_wait(barrier, n)
 
     def pack_copy(d):
         return pltpu.make_async_remote_copy(
-            src_ref=pack_send,
+            src_ref=pack_send.at[d],
             dst_ref=packs.at[d],
             send_sem=pack_ssem.at[d],
             recv_sem=pack_rsem.at[d],
-            device_id={"rows": lax.rem(me + d, n)},
+            device_id={"rows": partner(d)},
             device_id_type=MESH,
         )
 
-    def start_pack(d, carry):
-        pack_copy(d).start()
+    def start_pack(i, carry):
+        pack_copy(n - i).start()
         return carry
 
     lax.fori_loop(1, n, start_pack, 0)
 
-    copies[0].wait()
+    copies[4].wait()
     table_b[...] = table_v[...].astype(jnp.bfloat16)
-    copies[1].wait()
+    copies[2].wait()
+    copies[5].wait()
     fsend[...] = jnp.dot(
         own_ref[...].astype(jnp.bfloat16), ws_v[...], preferred_element_type=jnp.float32
     )
@@ -109,16 +147,13 @@
     lane = lax.broadcasted_iota(jnp.int32, (half_rows, LANES), 1)
     prow = lax.broadcasted_iota(jnp.int32, (half_rows, LANES), 0)
     t_of = (lax.rem(prow, 4) + jnp.where(lane >= HALF, 4, 0)).astype(jnp.float32)
-    base = (me * rows_dev).astype(jnp.float32)
 
     def build(d, slot):
-        ids = packs[d, pl.ds(0, half_rows), :]
-        weight = packs[d, pl.ds(half_rows, half_rows), :]
-        rel = ids - base
-        valid = jnp.logical_and(rel >= 0.0, rel < float(rows_dev))
+        rel = packs[d, pl.ds(0, half_rows), :].astype(jnp.int32).astype(jnp.float32)
+        weight = packs[d, pl.ds(half_rows, half_rows), :].astype(jnp.int32).astype(jnp.float32)
         high = jnp.floor(rel * (1.0 / LANES))
         low = rel - high * LANES
-        key = jnp.where(valid, high * SUB + t_of, -1.0)
+        key = jnp.where(rel >= 0.0, high * SUB + t_of, -1.0)
         for g in range(groups):
             lhs, rhs = [], []
             for c in range(4):
@@ -147,47 +182,47 @@
             dst_ref=precv.at[d],
             send_sem=part_ssem.at[d],
             recv_sem=part_rsem.at[d],
-            device_id={"rows": lax.rem(me - d + n, n)},
+            device_id={"rows": partner(d)},
             device_id_type=MESH,
         )
 
     def chunk(first, has_own):
         def one(s, carry):
-            d = first + s
+            d = first - s
             pack_copy(d).wait_recv()
             build(d, s)
             return carry
 
+        lax.fori_loop(0, peers_chunk - 1 if has_own else peers_chunk, one, 0)
         if has_own:
-            build(0, 0)
-        lax.fori_loop(1 if has_own else 0, peers_chunk, one, 0)
+            build(0, peers_chunk - 1)
         sums = jnp.dot(
             wmat[...].astype(jnp.bfloat16), table_b[...], preferred_element_type=jnp.float32
         )
         for s in range(peers_chunk):
             rows = sums[s * targets : (s + 1) * targets, :]
-            if has_own and s == 0:
+            if has_own and s == peers_chunk - 1:
                 mine[...] = rows
             else:
-                psend[first + s] = rows.astype(jnp.bfloat16)
-                part_copy(first + s).start()
-
-    chunk(0, True)
+                psend[first - s] = rows.astype(jnp.bfloat16)
+                part_copy(first - s).start()
 
     def later(i, carry):
-        chunk(i * peers_chunk, False)
-        return carry
-
-    lax.fori_loop(1, n // peers_chunk, later, 0)
-
-    def collect(d, carry):
+        chunk(n - 1 - i * peers_chunk, False)
+        return carry
+
+    lax.fori_loop(0, n // peers_chunk - 1, later, 0)
+    chunk(peers_chunk - 1, True)
+
+    def collect(i, carry):
+        d = n - i
         part_copy(d).wait_recv()
         mine[...] += precv[d].astype(jnp.float32)
         return carry
 
     lax.fori_loop(1, n, collect, 0)
-    pooled = mine[...] / jnp.sum(imp_ref[...], axis=1, keepdims=True)
-    copies[2].wait()
+    pooled = mine[...] / (IMP_SCALE * jnp.sum(imp_ref[...], axis=1, keepdims=True))
+    copies[6].wait()
     fsend[...] += jnp.dot(
         pooled.astype(jnp.bfloat16), wp_v[...], preferred_element_type=jnp.float32
     )
@@ -200,6 +235,7 @@
         device_id_type=MESH,
     )
     swap.start()
+    copies[3].wait()
     swap.wait_recv()
     hidden = jnp.maximum(fsend[...] + frecv[...] + bias_ref[...], 0.0)
     scale = lax.rsqrt(jnp.mean(hidden * hidden, axis=1, keepdims=True) + 1e-06)
@@ -222,28 +258,34 @@
     n = lax.axis_size("rows")
     full = w_self.shape[1]
     assert lax.axis_size("cols") == 2 and neigh <= HALF and targets % 16 == 0
-    peers_chunk = 4 if n % 4 == 0 else 1
+    assert n & (n - 1) == 0 and n > 1
+    peers_chunk = 2
     vmem = pl.BlockSpec(memory_space=pltpu.VMEM)
     hbm = pl.BlockSpec(memory_space=pl.ANY)
     return pl.pallas_call(
         partial(kernel, n, peers_chunk),
-        out_shape=jax.ShapeDtypeStruct((targets, width), jnp.float32),
-        in_specs=[vmem, vmem, vmem, vmem, hbm, hbm, hbm],
+        out_shape=pltpu.VMEM((targets, width), jnp.float32),
+        in_specs=[hbm] * 7,
         out_specs=vmem,
         scratch_shapes=[
+            pltpu.VMEM((targets, neigh), jnp.int32),
+            pltpu.VMEM((targets, neigh), jnp.float32),
+            pltpu.VMEM((targets, width), jnp.float32),
+            pltpu.VMEM((1, full), jnp.float32),
             pltpu.VMEM((rows_dev, width), jnp.float32),
             pltpu.VMEM((rows_dev, width), jnp.bfloat16),
             pltpu.VMEM(w_self.shape, jnp.bfloat16),
             pltpu.VMEM(w_pool.shape, jnp.bfloat16),
-            pltpu.VMEM((targets, LANES), jnp.float32),
-            pltpu.VMEM((n, targets, LANES), jnp.float32),
+            pltpu.VMEM((targets, LANES), jnp.int32),
+            pltpu.VMEM((n, targets, LANES), jnp.int16),
+            pltpu.VMEM((n, targets, LANES), jnp.int16),
             pltpu.VMEM((peers_chunk * targets, rows_dev), jnp.float32),
             pltpu.VMEM((targets, width), jnp.float32),
             pltpu.VMEM((n, targets, width), jnp.bfloat16),
             pltpu.VMEM((n, targets, width), jnp.bfloat16),
             pltpu.VMEM((targets, full), jnp.float32),
             pltpu.VMEM((targets, full), jnp.float32),
-            pltpu.SemaphoreType.DMA((3,)),
+            pltpu.SemaphoreType.DMA((7,)),
             pltpu.SemaphoreType.DMA((n,)),
             pltpu.SemaphoreType.DMA((n,)),
             pltpu.SemaphoreType.DMA((n,)),

time: 22.9 us -> 19.1 us (0.83)
  Pallas kernels: 21.3 us -> 18.2 us
  local copies, waits for them, and re-layouts: 1.47 us -> 0.63 us
    pallas_call x1, Pallas kernels: 21.3 us -> 18.2 us  [body(): pl.pallas_call(partial(kernel, n, peers_chunk), out_shape=pltpu.VMEM((tar...]
    unnamed x1, local copies, waits for them, and re-layouts: 1.47 us -> 0.63 us
where the time goes in v2:
time: 19.1 us; the launch traced here: 18.9 us
  Pallas kernels  18.2 us (95%)
  local copies, waits for them, and re-layouts  0.63 us (3%)
    pallas_call x1, Pallas kernels, body(): pl.pallas_call(partial(kernel, n, peers_chunk), out_shape=pltpu.VMEM((tar...  18.2 us
    unnamed x1, local copies, waits for them, and re-layouts  0.63 us

profile of v2, /device:TPU:0, one launch (start us, length us, event | category | flops | bytes accessed | tf_op | source)
XLA Modules:
  0.0 18.9 jit_solution(3160006140247535905)
XLA Ops:
  0.0 18.2 %shard_map.73 = f32[32,512]{1,0:T(8,128)S(1)} custom-call(s32[32,50]{1,0:T(8,128)} %ids_hbm.1, f32[32,50]{1,0:T(8,128)} %imp_hbm.1, f32[32,512]{1,0:T(8,128)} %own_hbm.1, f32[1,1024]{1,0:T(1,128)} %bitcast.1, f32[2048,512]{1,0:T(8,128)} %table_hbm.1, bf16[512,1024]{1,0:T(8,128)(2,1)} %ws_hbm.1, bf16[512,1024]{1,0:T(8,128)(2,1)} %wp_hbm.1), custom_call_target="tpu_custom_call" | custom-call | tf_op jit(solution)/shard_map/pallas_call | solution.py:265
  18.2 0.6 %copy.9 = f32[32,512]{1,0:T(8,128)} copy(f32[32,512]{1,0:T(8,128)S(1)} %shard_map.73) | data formatting | bytes 131072

commit v3 on v2

--- a/solution.py
+++ b/solution.py
@@ -47,7 +47,8 @@
     pack_rsem,
     part_ssem,
     part_rsem,
-    fin_sem,
+    fin_ssem,
+    fin_rsem,
 ):
     me = lax.axis_index("rows")
     col = lax.axis_index("cols")
@@ -59,21 +60,36 @@
 
     barrier = pltpu.get_barrier_semaphore()
 
+    flips, bit = [], 1
+    while bit < n:
+        flips.append((bit, (1 - 2 * lax.rem(lax.div(me, bit), 2)) * bit))
+        bit *= 2
+
     def partner(k):
-        peer, bit = me, 1
-        while bit < n:
-            peer = peer + lax.rem(k // bit, 2) * (1 - 2 * lax.rem(me // bit, 2)) * bit
-            bit *= 2
+        peer = me
+        for bit, flip in flips:
+            if isinstance(k, int):
+                peer = peer + flip if k // bit % 2 else peer
+            else:
+                peer = peer + lax.rem(lax.div(k, bit), 2) * flip
         return peer
 
-    def greet(d, carry):
+    def each(first, last, step):
+        if n <= 16:
+            for i in range(first, last):
+                step(i)
+        else:
+
+            def body(i, carry):
+                step(i)
+                return carry
+
+            lax.fori_loop(first, last, body, 0)
+
+    def greet(i):
         pl.semaphore_signal(
-            barrier, inc=1, device_id={"rows": partner(d)}, device_id_type=MESH
-        )
-        return carry
-
-    lax.fori_loop(1, n, greet, 0)
-    pl.semaphore_signal(barrier, inc=1, device_id={"cols": 1 - col}, device_id_type=MESH)
+            barrier, inc=1, device_id={"rows": partner(n - i)}, device_id_type=MESH
+        )
 
     copies = tuple(
         pltpu.make_async_copy(src, dst, local_sem.at[i])
@@ -89,7 +105,11 @@
             )
         )
     )
-    for c in copies:
+    copies[0].start()
+    copies[1].start()
+    each(1, n, greet)
+    pl.semaphore_signal(barrier, inc=1, device_id={"cols": 1 - col}, device_id_type=MESH)
+    for c in copies[2:]:
         c.start()
     copies[0].wait()
     copies[1].wait()
@@ -104,16 +124,15 @@
                 imp_ref[src, :] * IMP_SCALE
             ).astype(jnp.int32)
 
-    def pack_for(k, carry):
+    def pack_for(k):
         local = pack_in[pl.ds(0, half_rows), :] - partner(k) * rows_dev
         local = jnp.where(jnp.logical_and(local >= 0, local < rows_dev), local, -1)
         pack_send[k, pl.ds(0, half_rows), :] = local.astype(jnp.int16)
         pack_send[k, pl.ds(half_rows, half_rows), :] = pack_in[
             pl.ds(half_rows, half_rows), :
         ].astype(jnp.int16)
-        return carry
-
-    lax.fori_loop(0, n, pack_for, 0)
+
+    each(0, n, pack_for)
     packs[0] = pack_send[0]
 
     pl.semaphore_wait(barrier, n)
@@ -128,19 +147,17 @@
             device_id_type=MESH,
         )
 
-    def start_pack(i, carry):
-        pack_copy(n - i).start()
-        return carry
-
-    lax.fori_loop(1, n, start_pack, 0)
+    each(1, n, lambda i: pack_copy(n - i).start())
 
     copies[4].wait()
     table_b[...] = table_v[...].astype(jnp.bfloat16)
     copies[2].wait()
     copies[5].wait()
-    fsend[...] = jnp.dot(
-        own_ref[...].astype(jnp.bfloat16), ws_v[...], preferred_element_type=jnp.float32
-    )
+    own = own_ref[...].astype(jnp.bfloat16)
+    for h in range(2):
+        fsend[h] = jnp.dot(
+            own, ws_v[:, h * width : (h + 1) * width], preferred_element_type=jnp.float32
+        )
 
     row_iota = lax.broadcasted_iota(jnp.int32, (LANES, LANES), 0).astype(jnp.float32)
     key_iota = lax.broadcasted_iota(jnp.int32, (hi_count * SUB, LANES), 0).astype(jnp.float32)
@@ -193,9 +210,9 @@
             build(d, s)
             return carry
 
-        lax.fori_loop(0, peers_chunk - 1 if has_own else peers_chunk, one, 0)
         if has_own:
             build(0, peers_chunk - 1)
+        lax.fori_loop(0, peers_chunk - 1 if has_own else peers_chunk, one, 0)
         sums = jnp.dot(
             wmat[...].astype(jnp.bfloat16), table_b[...], preferred_element_type=jnp.float32
         )
@@ -207,49 +224,53 @@
                 psend[first - s] = rows.astype(jnp.bfloat16)
                 part_copy(first - s).start()
 
-    def later(i, carry):
-        chunk(n - 1 - i * peers_chunk, False)
-        return carry
-
-    lax.fori_loop(0, n // peers_chunk - 1, later, 0)
     chunk(peers_chunk - 1, True)
-
-    def collect(i, carry):
+    each(0, n // peers_chunk - 1, lambda i: chunk(n - 1 - i * peers_chunk, False))
+    inverse = 1.0 / (IMP_SCALE * jnp.sum(imp_ref[...], axis=1, keepdims=True))
+    copies[6].wait()
+    copies[3].wait()
+
+    def collect(i):
         d = n - i
         part_copy(d).wait_recv()
         mine[...] += precv[d].astype(jnp.float32)
-        return carry
-
-    lax.fori_loop(1, n, collect, 0)
-    pooled = mine[...] / (IMP_SCALE * jnp.sum(imp_ref[...], axis=1, keepdims=True))
-    copies[6].wait()
-    fsend[...] += jnp.dot(
-        pooled.astype(jnp.bfloat16), wp_v[...], preferred_element_type=jnp.float32
-    )
-    swap = pltpu.make_async_remote_copy(
-        src_ref=fsend,
-        dst_ref=frecv,
-        send_sem=fin_sem.at[0],
-        recv_sem=fin_sem.at[1],
-        device_id={"cols": 1 - col},
-        device_id_type=MESH,
-    )
-    swap.start()
-    copies[3].wait()
-    swap.wait_recv()
-    hidden = jnp.maximum(fsend[...] + frecv[...] + bias_ref[...], 0.0)
-    scale = lax.rsqrt(jnp.mean(hidden * hidden, axis=1, keepdims=True) + 1e-06)
-    half = jnp.where(col == 0, hidden[:, :width], hidden[:, width:])
-    out_ref[...] = half * scale
-
-    swap.wait_send()
-
-    def drain(d, carry):
+
+    each(1, n, collect)
+    pooled = (mine[...] * inverse).astype(jnp.bfloat16)
+
+    def swap(h):
+        return pltpu.make_async_remote_copy(
+            src_ref=fsend.at[h],
+            dst_ref=frecv.at[h],
+            send_sem=fin_ssem.at[h],
+            recv_sem=fin_rsem.at[h],
+            device_id={"cols": 1 - col},
+            device_id_type=MESH,
+        )
+
+    for h in range(2):
+        fsend[h] += jnp.dot(
+            pooled, wp_v[:, h * width : (h + 1) * width], preferred_element_type=jnp.float32
+        )
+        swap(h).start()
+    hidden = []
+    for h in range(2):
+        swap(h).wait_recv()
+        hidden.append(
+            jnp.maximum(fsend[h] + frecv[h] + bias_ref[:, h * width : (h + 1) * width], 0.0)
+        )
+    square = jnp.sum(hidden[0] * hidden[0] + hidden[1] * hidden[1], axis=1, keepdims=True)
+    scale = lax.rsqrt(square * (0.5 / width) + 1e-06)
+    out_ref[...] = jnp.where(col == 0, hidden[0], hidden[1]) * scale
+
+    swap(0).wait_send()
+    swap(1).wait_send()
+
+    def drain(d):
         pack_copy(d).wait_send()
         part_copy(d).wait_send()
-        return carry
-
-    lax.fori_loop(1, n, drain, 0)
+
+    each(1, n, drain)
 
 
 def body(feature_table, own_features, neighbor_ids, importance, w_self, w_pool, bias):
@@ -257,7 +278,7 @@
     targets, neigh = neighbor_ids.shape
     n = lax.axis_size("rows")
     full = w_self.shape[1]
-    assert lax.axis_size("cols") == 2 and neigh <= HALF and targets % 16 == 0
+    assert lax.axis_size("cols") == 2 and full == 2 * width and neigh <= HALF and targets % 16 == 0
     assert n & (n - 1) == 0 and n > 1
     peers_chunk = 2
     vmem = pl.BlockSpec(memory_space=pltpu.VMEM)
@@ -283,13 +304,14 @@
             pltpu.VMEM((targets, width), jnp.float32),
             pltpu.VMEM((n, targets, width), jnp.bfloat16),
             pltpu.VMEM((n, targets, width), jnp.bfloat16),
-            pltpu.VMEM((targets, full), jnp.float32),
-            pltpu.VMEM((targets, full), jnp.float32),
+            pltpu.VMEM((2, targets, width), jnp.float32),
+            pltpu.VMEM((2, targets, width), jnp.float32),
             pltpu.SemaphoreType.DMA((7,)),
             pltpu.SemaphoreType.DMA((n,)),
             pltpu.SemaphoreType.DMA((n,)),
             pltpu.SemaphoreType.DMA((n,)),
             pltpu.SemaphoreType.DMA((n,)),
+            pltpu.SemaphoreType.DMA((2,)),
             pltpu.SemaphoreType.DMA((2,)),
         ],
         compiler_params=pltpu.CompilerParams(collective_id=0, has_side_effects=True),

time: 19.1 us -> 19.1 us (level)
  no operation moved by 1% of the time
where the time goes in v3:
time: 19.1 us; the launch traced here: 18.8 us
  Pallas kernels  18.2 us (95%)
  local copies, waits for them, and re-layouts  0.63 us (3%)
    pallas_call x1, Pallas kernels, body(): pl.pallas_call(partial(kernel, n, peers_chunk), out_shape=pltpu.VMEM((tar...  18.2 us
    unnamed x1, local copies, waits for them, and re-layouts  0.63 us

profile of v3, /device:TPU:0, one launch (start us, length us, event | category | flops | bytes accessed | tf_op | source)
XLA Modules:
  0.0 18.8 jit_solution(4377506995368419693)
XLA Ops:
  0.0 18.2 %shard_map.73 = f32[32,512]{1,0:T(8,128)S(1)} custom-call(s32[32,50]{1,0:T(8,128)} %ids_hbm.1, f32[32,50]{1,0:T(8,128)} %imp_hbm.1, f32[32,512]{1,0:T(8,128)} %own_hbm.1, f32[1,1024]{1,0:T(1,128)} %bitcast.1, f32[2048,512]{1,0:T(8,128)} %table_hbm.1, bf16[512,1024]{1,0:T(8,128)(2,1)} %ws_hbm.1, bf16[512,1024]{1,0:T(8,128)(2,1)} %wp_hbm.1), custom_call_target="tpu_custom_call" | custom-call | tf_op jit(solution)/shard_map/pallas_call | solution.py:286
  18.2 0.6 %copy.9 = f32[32,512]{1,0:T(8,128)} copy(f32[32,512]{1,0:T(8,128)S(1)} %shard_map.73) | data formatting | bytes 131072
